TPU v7x, 32 devices: a whole 2x2x4 slice. The times are simulated.
32 devices in a mesh: seq: 8 (over z, y), tp: 4 (over x, core).
Axes of the slice: x: 2, y: 2, z: 4, core: 2. Of those that a mesh axis runs over, the one named last changes fastest.
Arguments:
- inputs: bfloat16 [2, 32, 8192], P(None, 'seq', 'tp'), may hold values from -6 to 6
- out_grad: bfloat16 [2, 32, 8192], P(None, 'seq', 'tp'), may hold values from -6 to 6
- gate_weight: bfloat16 [8192, 14848], P('tp', 'seq'), may hold values from -0.0625 to 0.0625
- up_weight: bfloat16 [8192, 14848], P('tp', 'seq'), may hold values from -0.0625 to 0.0625
- down_weight: bfloat16 [14848, 8192], P('seq', 'tp'), may hold values from -0.0625 to 0.0625
Outputs:
- input_grad: bfloat16 [2, 32, 8192], P(None, 'seq', 'tp')
- gate_grad: float32 [8192, 14848], P('tp', 'seq')
- up_grad: float32 [8192, 14848], P('tp', 'seq')
- down_grad: float32 [14848, 8192], P('seq', 'tp')
All inputs are finite; a program needn't handle non-finite values.
Results may differ from a plain program's by a relative error of at most 0.0049.
Values may be sent and summed in bfloat16 or wider, within the bound.
A program may use at most 128 MiB of HBM per device.

v0:
```python
import functools

import jax
import jax.numpy as jnp
from jax import lax
from jax.experimental import pallas as pl
from jax.experimental.pallas import tpu as pltpu
from jax.sharding import PartitionSpec as P

MESH = pl.DeviceIdType.MESH
F32 = jnp.float32
BF16 = jnp.bfloat16
NT = (((1,), (1,)), ((), ()))
TILE = 256


def tiles_of(size, tile, body):
    whole = size // tile

    @pl.loop(0, whole)
    def _(i):
        body(pl.multiple_of(i * tile, tile), tile)

    if size % tile:
        body(whole * tile, size % tile)


def front_kernel(n_seq, n_tp, x_ref, dy_ref, wg_hbm, wu_hbm, wd_hbm,
                 x_out, dy_out, hid_out, gu_out, uu_out, ig_out,
                 gath, wg, wu, wd, part, from_core, chip_sum, sendx, from_chip, acts,
                 w_sem, z_send, z_recv, y_send, y_recv,
                 c_send, c_recv, r_send, r_recv, a_send, a_recv, f_send, f_recv):
    seq = lax.axis_index("seq")
    tp = lax.axis_index("tp")
    nz, nchip = n_seq // 2, n_tp // 2
    z, y = seq // 2, lax.rem(seq, 2)
    chip, core = tp // 2, lax.rem(tp, 2)
    tokens = hid_out.shape[0]
    ffw = wg_hbm.shape[0]
    share = tokens // n_tp
    at_y = {"seq": z * 2 + (1 - y)}
    at_core = {"tp": chip * 2 + (1 - core)}

    def z_at(k):
        return lax.rem(z + k, nz)

    def chip_at(k):
        return lax.rem(chip + k, nchip)

    loads = [
        pltpu.make_async_copy(src, dst, w_sem.at[i])
        for i, (src, dst) in enumerate(((wg_hbm, wg), (wu_hbm, wu), (wd_hbm, wd)))
    ]
    for load in loads:
        load.start()

    barrier = pltpu.get_barrier_semaphore()
    for k in range(1, nz):
        pl.semaphore_signal(barrier, inc=1, device_id={"seq": z_at(k) * 2 + y}, device_id_type=MESH)
    for k in range(1, nchip):
        pl.semaphore_signal(barrier, inc=1, device_id={"tp": chip_at(k) * 2 + core}, device_id_type=MESH)
    pl.semaphore_signal(barrier, inc=1, device_id=at_y, device_id_type=MESH)
    pl.semaphore_signal(barrier, inc=1, device_id=at_core, device_id_type=MESH)
    pl.semaphore_wait(barrier, nz - 1 + nchip - 1 + 2)

    def remote(src, dst, send, recv, to):
        return pltpu.make_async_remote_copy(
            src_ref=src, dst_ref=dst, send_sem=send, recv_sem=recv, device_id=to, device_id_type=MESH
        )

    z_copies, y_copies = [], []
    for a, ref in enumerate((x_ref, dy_ref)):
        own = [
            remote(ref, gath.at[a, z, y], z_send.at[a, k], z_recv.at[a, k], {"seq": z_at(k) * 2 + y})
            for k in range(1, nz)
        ]
        over = [remote(ref, gath.at[a, z, y], y_send.at[a, 0], y_recv.at[a, 0], at_y)]
        over += [
            remote(gath.at[a, z_at(nz - k), y], gath.at[a, z_at(nz - k), y],
                   y_send.at[a, k], y_recv.at[a, k], at_y)
            for k in range(1, nz)
        ]
        z_copies.append(own)
        y_copies.append(over)
    for a in range(2):
        y_copies[a][0].start()
        for copy in z_copies[a]:
            copy.start()
    for a, ref in enumerate((x_ref, dy_ref)):
        gath[a, z, y] = ref[...]

    def forward(a):
        for k in range(1, nz):
            z_copies[a][k - 1].wait_recv()
            y_copies[a][k].start()

    def arrive(a, out):
        for k in range(nz):
            y_copies[a][k].wait_recv()
        out[...] = gath[a].astype(F32).reshape(out.shape).astype(BF16)

    c_copies = [
        remote(part.at[q, :, 1 - core], from_core.at[q], c_send.at[q], c_recv.at[q], at_core)
        for q in range(3)
    ]
    r_copies = [
        [
            remote(sendx.at[q, k - 1], from_chip.at[q, k - 1], r_send.at[q, k], r_recv.at[q, k],
                   {"tp": chip_at(k) * 2 + core})
            for k in range(1, nchip)
        ]
        for q in range(3)
    ]

    def product(q, out, w):
        def body(start, width):
            val = lax.dot_general(out[...], w[pl.ds(start, width), :], NT, preferred_element_type=F32)
            part[q, :, :, :, pl.ds(start, width)] = val.reshape(nchip, 2, share, width)

        tiles_of(ffw, TILE, body)
        c_copies[q].start()

    def reduce_chip(q):
        c_copies[q].wait_recv()
        for k in range(1, nchip):
            sendx[q, k - 1] = (part[q, chip_at(k), core] + from_core[q, chip_at(k)]).astype(BF16)
            r_copies[q][k - 1].start()
        chip_sum[q] = part[q, chip, core] + from_core[q, chip]

    forward(0)
    arrive(0, x_out)
    loads[0].wait()
    product(0, x_out, wg)
    forward(1)
    loads[1].wait()
    product(1, x_out, wu)
    reduce_chip(0)
    reduce_chip(1)
    arrive(1, dy_out)
    loads[2].wait()
    product(2, dy_out, wd)
    reduce_chip(2)
    for q in range(3):
        for k in range(1, nchip):
            r_copies[q][k - 1].wait_recv()

    def total(q):
        value = chip_sum[q]
        for k in range(1, nchip):
            value = value + from_chip[q, k - 1].astype(F32)
        return value

    gate, up, grad = total(0), total(1), total(2)
    sig = jax.nn.sigmoid(gate)
    acts[0, chip, core] = (grad * up * sig * (1.0 + gate * (1.0 - sig))).astype(BF16)
    acts[1, chip, core] = (grad * gate * sig).astype(BF16)
    acts[2, chip, core] = (gate * sig * up).astype(BF16)

    a_copies, f_copies = [], []
    for q in range(3):
        mine = acts.at[q, chip, core]
        a_copies.append([
            remote(mine, mine, a_send.at[q, k], a_recv.at[q, k], {"tp": chip_at(k) * 2 + core})
            for k in range(1, nchip)
        ])
        over = [remote(mine, mine, f_send.at[q, 0], f_recv.at[q, 0], at_core)]
        for k in range(1, nchip):
            theirs = acts.at[q, chip_at(nchip - k), core]
            over.append(remote(theirs, theirs, f_send.at[q, k], f_recv.at[q, k], at_core))
        f_copies.append(over)
    for q in range(3):
        for copy in a_copies[q]:
            copy.start()
        f_copies[q][0].start()
    outs = (gu_out, uu_out, hid_out)

    def settle(q):
        for k in range(1, nchip):
            a_copies[q][k - 1].wait_recv()
            f_copies[q][k].start()

    def collect(q):
        for k in range(nchip):
            f_copies[q][k].wait_recv()
        if outs[q].shape[1] > ffw:
            start = ffw // 128 * 128
            outs[q][:, start:] = jnp.zeros((tokens, outs[q].shape[1] - start), BF16)
        outs[q][:, :ffw] = acts[q].reshape(tokens, ffw)

    def back(q, w):
        def body(start, width):
            val = jnp.dot(outs[q][:, :ffw], w[:, pl.ds(start, width)], preferred_element_type=F32)
            if q:
                val = val + ig_out[:, pl.ds(start, width)]
            ig_out[:, pl.ds(start, width)] = val

        tiles_of(ig_out.shape[1], TILE, body)

    settle(0)
    settle(1)
    collect(0)
    back(0, wg)
    settle(2)
    collect(1)
    back(1, wu)
    collect(2)

    for a in range(2):
        for copy in z_copies[a] + y_copies[a]:
            copy.wait_send()
    for q in range(3):
        for copy in [c_copies[q]] + r_copies[q] + a_copies[q] + f_copies[q]:
            copy.wait_send()


def front(n_seq, n_tp, x, dy, wg, wu, wd):
    rows, width = x.shape
    ffw = wg.shape[0]
    padded = pl.cdiv(ffw, TILE) * TILE
    tokens = rows * n_seq
    nz, nchip = n_seq // 2, n_tp // 2
    share = tokens // n_tp
    vmem = pl.BlockSpec(memory_space=pltpu.VMEM)
    hbm = pl.BlockSpec(memory_space=pl.ANY)
    dma = pltpu.SemaphoreType.DMA
    others = max(nchip - 1, 1)
    return pl.pallas_call(
        functools.partial(front_kernel, n_seq, n_tp),
        out_shape=[jax.ShapeDtypeStruct((tokens, width), BF16)] * 2
        + [jax.ShapeDtypeStruct((tokens, padded), BF16)] * 3
        + [jax.ShapeDtypeStruct((tokens, width), F32)],
        in_specs=[vmem, vmem, hbm, hbm, hbm],
        out_specs=[vmem] * 6,
        scratch_shapes=[
            pltpu.VMEM((2, nz, 2, rows, width), BF16),
            pltpu.VMEM(wg.shape, BF16),
            pltpu.VMEM(wu.shape, BF16),
            pltpu.VMEM(wd.shape, BF16),
            pltpu.VMEM((3, nchip, 2, share, ffw), F32),
            pltpu.VMEM((3, nchip, share, ffw), F32),
            pltpu.VMEM((3, share, ffw), F32),
            pltpu.VMEM((3, others, share, ffw), BF16),
            pltpu.VMEM((3, others, share, ffw), BF16),
            pltpu.VMEM((3, nchip, 2, share, ffw), BF16),
            dma((3,)),
            dma((2, nz)), dma((2, nz)), dma((2, nz)), dma((2, nz)),
            dma((3,)), dma((3,)),
            dma((3, nchip)), dma((3, nchip)),
            dma((3, nchip)), dma((3, nchip)), dma((3, nchip)), dma((3, nchip)),
        ],
        compiler_params=pltpu.CompilerParams(
            collective_id=0, has_side_effects=True, vmem_limit_bytes=48 * 1024 * 1024
        ),
        cost_estimate=pl.CostEstimate(
            flops=10 * tokens * width * ffw, bytes_accessed=6 * width * ffw, transcendentals=0
        ),
    )(x, dy, wg, wu, wd)


def weight_kernel(pairs, *refs):
    lefts, right, outs = refs[:pairs], refs[pairs], refs[pairs + 1 :]
    columns = pl.ds(pl.multiple_of(pl.program_id(0) * TILE, TILE), TILE)
    for left, out in zip(lefts, outs):
        turned = left[:, columns].astype(F32).T.astype(BF16)
        out[...] = jnp.dot(turned, right[...], preferred_element_type=F32)


def weight_grads(rows, lefts, right):
    tokens, width = right.shape
    pairs = len(lefts)
    return pl.pallas_call(
        functools.partial(weight_kernel, pairs),
        grid=(pl.cdiv(rows, TILE),),
        out_shape=[jax.ShapeDtypeStruct((rows, width), F32)] * pairs,
        in_specs=[pl.BlockSpec(memory_space=pltpu.VMEM)] * (pairs + 1),
        out_specs=[pl.BlockSpec((TILE, width), lambda i: (i, 0))] * pairs,
        cost_estimate=pl.CostEstimate(
            flops=2 * pairs * tokens * rows * width,
            bytes_accessed=4 * pairs * rows * width,
            transcendentals=0,
        ),
    )(*lefts, right)


def scatter_sum(n_seq, partial, cover):
    nz = n_seq // 2
    seq = lax.axis_index("seq")
    z, y = seq // 2, lax.rem(seq, 2)
    rows = partial.shape[0] // n_seq
    pieces = partial.reshape(nz, 2, rows, partial.shape[1])
    away = lax.dynamic_index_in_dim(pieces, 1 - y, 1, keepdims=False)
    kept = lax.dynamic_index_in_dim(pieces, y, 1, keepdims=False)
    arrived = lax.ppermute(away, "seq", [(i, i ^ 1) for i in range(n_seq)])
    kept, *cover = lax.optimization_barrier((kept, *cover))
    summed = kept + arrived
    result = lax.dynamic_index_in_dim(summed, z, 0, keepdims=False)
    for k in range(1, nz):
        send = lax.dynamic_index_in_dim(summed, lax.rem(z + k, nz), 0, keepdims=False)
        result = result + lax.ppermute(
            send, "seq", [(i, (i + 2 * k) % n_seq) for i in range(n_seq)]
        )
    return result, cover


def solution(mesh):
    n_seq, n_tp = mesh.shape["seq"], mesh.shape["tp"]

    def per_device(inputs, out_grad, gate_weight, up_weight, down_weight):
        blocks, rows, width = inputs.shape
        x, dy, hidden, gate_unit, up_unit, partial = front(
            n_seq, n_tp,
            inputs.reshape(blocks * rows, width), out_grad.reshape(blocks * rows, width),
            gate_weight.T, up_weight.T, down_weight,
        )
        hidden_units = down_weight.shape[0]
        cover = weight_grads(hidden_units, (gate_unit, up_unit), x)
        total, (gate_grad, up_grad) = scatter_sum(n_seq, partial, cover)
        (down_grad,) = weight_grads(hidden_units, (hidden,), dy)
        return total.astype(BF16).reshape(inputs.shape), gate_grad.T, up_grad.T, down_grad

    return jax.shard_map(
        per_device,
        mesh=mesh,
        in_specs=(
            P(None, "seq", "tp"),
            P(None, "seq", "tp"),
            P("tp", "seq"),
            P("tp", "seq"),
            P("seq", "tp"),
        ),
        out_specs=(P(None, "seq", "tp"), P("tp", "seq"), P("tp", "seq"), P("seq", "tp")),
        check_vma=False,
    )
```

profile of v0, /device:TPU:0, one launch (start us, length us, event | category | flops | bytes accessed | tf_op | source)
XLA Modules:
  0.0 69.7 jit_solution(12596748421899042372)
XLA Ops:
  0.6 0.8 %reshape.20.x_ref = bf16[8,2048]{1,0:T(8,128)(2,1)S(1)} reshape(bf16[2,4,2048]{2,1,0:T(4,128)(2,1)} %param.5) | data formatting | bytes 65536 | tf_op jit(solution)/shard_map/reshape | solution.py:312
  1.4 0.8 %reshape.21.dy_ref = bf16[8,2048]{1,0:T(8,128)(2,1)S(1)} reshape(bf16[2,4,2048]{2,1,0:T(4,128)(2,1)} %param.6) | data formatting | bytes 65536 | tf_op jit(solution)/shard_map/reshape | solution.py:312
  2.2 39.3 %shard_map.84 = (bf16[64,2048]{1,0:T(8,128)(2,1)S(1)}, bf16[64,2048]{1,0:T(8,128)(2,1)S(1)}, bf16[64,2048]{1,0:T(8,128)(2,1)S(1)}, bf16[64,2048]{1,0:T(8,128)(2,...) custom-call(bf16[8,2048]{1,0:T(8,128)(2,1)S(1)} %reshape.20.x_ref, bf16[8,2048]{1,0:T(8,128)(2,1)S(1)} %reshape.21.dy_ref, ...), custom_call_target="tpu_custom_call" | custom-call | flops 2432696320 | bytes 22806528 | tf_op jit(solution)/shard_map/pallas_call | solution.py:227
  41.5 0.0 copy-start.4
  41.5 0.7 copy-done.4
  42.2 0.0 copy-start
  42.2 0.0 copy-start.1
  42.2 0.0 copy-start.2
  42.2 0.0 copy-start.3
  42.2 0.7 copy-done
  42.9 0.1 copy-done.1
  43.0 0.1 copy-done.2
  43.1 0.1 copy-done.3
  43.1 0.7 collective-permute-start
  43.8 12.3 %shard_map.85 = (f32[1856,2048]{1,0:T(8,128)}, f32[1856,2048]{1,0:T(8,128)}) custom-call(bf16[64,2048]{1,0:T(8,128)(2,1)} %copy-done.3, bf16[64,2048]{1,0:T(8,128)(2,1)} %copy-done.4, bf16[64,2048]{1,0:T(8,128)(2,1)} %copy-done.2), custom_call_target="tpu_custom_call" | custom-call | flops 973078528 | bytes 30408704 | tf_op jit(solution)/shard_map/pallas_call | solution.py:271
  56.1 0.0 collective-permute-done
  56.1 2.0 %collective-permute-start.1 = (f32[8,2048]{1,0:T(8,128)S(1)}, f32[8,2048]{1,0:T(8,128)S(1)}, u32[]{:S(2)}, u32[]{:S(2)}) collective-permute-start(f32[8,2048]{1,0:T(8,128)S(1)} %get-tuple-element.28), channel_id=1, source_target_pairs={{0,8},{4,12},{8,16},{12,20},{16,24},{20,28},{24,0},{28,4},{1,9},{5... | collective-permute-start | bytes 196616 | tf_op jit(solution)/shard_map/ppermute | solution.py:299
  58.2 1.3 %collective-permute-start.2 = (f32[8,2048]{1,0:T(8,128)S(1)}, f32[8,2048]{1,0:T(8,128)S(1)}, u32[]{:S(2)}, u32[]{:S(2)}) collective-permute-start(f32[8,2048]{1,0:T(8,128)S(1)} %get-tuple-element.30), channel_id=1, source_target_pairs={{0,16},{4,20},{8,24},{12,28},{16,0},{20,4},{24,8},{28,12},{1,17},{... | collective-permute-start | bytes 196616 | tf_op jit(solution)/shard_map/ppermute | solution.py:299
  59.5 1.1 %collective-permute-start.3 = (f32[8,2048]{1,0:T(8,128)S(1)}, f32[8,2048]{1,0:T(8,128)S(1)}, u32[]{:S(2)}, u32[]{:S(2)}) collective-permute-start(f32[8,2048]{1,0:T(8,128)S(1)} %get-tuple-element.29), channel_id=1, source_target_pairs={{0,24},{4,28},{8,0},{12,4},{16,8},{20,12},{24,16},{28,20},{1,25},{... | collective-permute-start | bytes 196616 | tf_op jit(solution)/shard_map/ppermute | solution.py:299
  60.6 8.4 %shard_map.86 = f32[1856,2048]{1,0:T(8,128)} custom-call(bf16[64,2048]{1,0:T(8,128)(2,1)} %copy-done.1, bf16[64,2048]{1,0:T(8,128)(2,1)} %copy-done), custom_call_target="tpu_custom_call" | custom-call | flops 486539264 | bytes 15204352 | tf_op jit(solution)/shard_map/pallas_call | solution.py:271
  69.0 0.0 collective-permute-done.1
  69.0 0.0 collective-permute-done.2
  69.0 0.0 collective-permute-done.3
  69.0 0.6 reshape.23
  (4 shorter events, 0.1 us)
Async XLA Ops:
  41.5 0.7 copy-start.4
  42.2 0.7 %copy-start = (bf16[64,2048]{1,0:T(8,128)(2,1)}, bf16[64,2048]{1,0:T(8,128)(2,1)S(1)}, u32[]{:S(2)}) copy-start(bf16[64,2048]{1,0:T(8,128)(2,1)S(1)} %get-tuple-element.25.refs_1_) | copy-start | bytes 786436
  42.2 0.8 %copy-start.1 = (bf16[64,2048]{1,0:T(8,128)(2,1)}, bf16[64,2048]{1,0:T(8,128)(2,1)S(1)}, u32[]{:S(2)}) copy-start(bf16[64,2048]{1,0:T(8,128)(2,1)S(1)} %get-tuple-element.24.refs_0_) | copy-start | bytes 786436
  42.2 0.9 %copy-start.2 = (bf16[64,2048]{1,0:T(8,128)(2,1)}, bf16[64,2048]{1,0:T(8,128)(2,1)S(1)}, u32[]{:S(2)}) copy-start(bf16[64,2048]{1,0:T(8,128)(2,1)S(1)} %get-tuple-element.18.refs_2_) | copy-start | bytes 786436
  42.2 1.0 %copy-start.3 = (bf16[64,2048]{1,0:T(8,128)(2,1)}, bf16[64,2048]{1,0:T(8,128)(2,1)S(1)}, u32[]{:S(2)}) copy-start(bf16[64,2048]{1,0:T(8,128)(2,1)S(1)} %get-tuple-element.16.refs_0_) | copy-start | bytes 786436
  43.1 12.9 %collective-permute-start = (f32[4,8,2048]{2,1,0:T(8,128)S(1)}, f32[4,8,2048]{2,1,0:T(8,128)S(1)}, u32[]{:S(2)}, u32[]{:S(2)}) collective-permute-start(f32[4,8,2048]{2,1,0:T(8,128)S(1)} %get-tuple-element.26), channel_id=1, source_target_pairs={{0,4},{4,0},{8,12},{12,8},{16,20},{20,16},{24,28},{28,24},{1,5},{5... | collective-permute-start | bytes 786440 | tf_op jit(solution)/shard_map/ppermute | solution.py:293
  56.1 12.8 %collective-permute-start.1 = (f32[8,2048]{1,0:T(8,128)S(1)}, f32[8,2048]{1,0:T(8,128)S(1)}, u32[]{:S(2)}, u32[]{:S(2)}) collective-permute-start(f32[8,2048]{1,0:T(8,128)S(1)} %get-tuple-element.28), channel_id=1, source_target_pairs={{0,8},{4,12},{8,16},{12,20},{16,24},{20,28},{24,0},{28,4},{1,9},{5... | collective-permute-start | bytes 196616 | tf_op jit(solution)/shard_map/ppermute | solution.py:299
  58.2 10.8 %collective-permute-start.2 = (f32[8,2048]{1,0:T(8,128)S(1)}, f32[8,2048]{1,0:T(8,128)S(1)}, u32[]{:S(2)}, u32[]{:S(2)}) collective-permute-start(f32[8,2048]{1,0:T(8,128)S(1)} %get-tuple-element.30), channel_id=1, source_target_pairs={{0,16},{4,20},{8,24},{12,28},{16,0},{20,4},{24,8},{28,12},{1,17},{... | collective-permute-start | bytes 196616 | tf_op jit(solution)/shard_map/ppermute | solution.py:299
  59.5 9.5 %collective-permute-start.3 = (f32[8,2048]{1,0:T(8,128)S(1)}, f32[8,2048]{1,0:T(8,128)S(1)}, u32[]{:S(2)}, u32[]{:S(2)}) collective-permute-start(f32[8,2048]{1,0:T(8,128)S(1)} %get-tuple-element.29), channel_id=1, source_target_pairs={{0,24},{4,28},{8,0},{12,4},{16,8},{20,12},{24,16},{28,20},{1,25},{... | collective-permute-start | bytes 196616 | tf_op jit(solution)/shard_map/ppermute | solution.py:299
where the time goes:
time: 69.9 us; the launch traced here: 69.7 us
  Pallas kernels  59.9 us (86%)
  starting transfers between devices  5.13 us (7%)
  local copies, waits for them, and re-layouts  3.83 us (5%)
  between operations  0.7 us (1%)
    pallas_call x1, Pallas kernels, front(): pl.pallas_call(functools.partial(front_kernel, n_seq, n_tp), out_shape=[j...  39.3 us
    pallas_call x2, Pallas kernels, weight_grads(): pl.pallas_call(functools.partial(weight_kernel, pairs), grid=(pl.cdiv(row...  20.6 us
    ppermute x3, starting transfers between devices, scatter_sum(): lax.ppermute(send, 'seq', [(i, (i + 2 * k) % n_seq) for i in range(n_seq)])  4.47 us
    unnamed x10, local copies, waits for them, and re-layouts  1.58 us
  transfers between devices with their start and end apart: 4, of which 0 were waited for; matrix products, arithmetic and copies ran while one was open for 0% of the time, Pallas kernels for 30%

commit v1 on v0

v1 whole, which is shorter than its diff:
```python
import functools

import jax
import jax.numpy as jnp
from jax import lax
from jax.experimental import pallas as pl
from jax.experimental.pallas import tpu as pltpu
from jax.sharding import PartitionSpec as P

MESH = pl.DeviceIdType.MESH
F32 = jnp.float32
BF16 = jnp.bfloat16
NT = (((1,), (1,)), ((), ()))
CHUNK = 512
LAG = 2


def padded(size):
    return pl.cdiv(size, 128) * 128


def chunks_of(ffw):
    return [(start, min(CHUNK, ffw - start)) for start in range(0, ffw, CHUNK)]


def front_kernel(n_seq, n_tp, x_hbm, dy_hbm, wg_hbm, wu_hbm, wd_hbm,
                 x_out, dy_out, gu_out, uu_out, hid_out, ig_out,
                 raw, own, gath, wg, wu, wd, part, from_core, sendx, from_chip, acts,
                 in_sem, w_sem, z_send, z_recv, y_send, y_recv,
                 c_send, c_recv, r_send, r_recv, f_send, f_recv):
    seq = lax.axis_index("seq")
    tp = lax.axis_index("tp")
    nz, nchip = n_seq // 2, n_tp // 2
    z, y = lax.div(seq, 2), lax.rem(seq, 2)
    chip, core = lax.div(tp, 2), lax.rem(tp, 2)
    blocks, lines = x_hbm.shape[:2]
    ffw = wg_hbm.shape[0]
    half = gu_out.shape[0] // 2
    chunks = chunks_of(ffw)
    weights = (wg, wu, wd)
    at_y = {"seq": z * 2 + (1 - y)}
    at_core = {"tp": chip * 2 + (1 - core)}

    def z_at(k):
        return lax.rem(z + k, nz)

    def chip_at(k):
        return lax.rem(chip + k, nchip)

    reads = [
        pltpu.make_async_copy(src, raw.at[a], in_sem.at[a]) for a, src in enumerate((x_hbm, dy_hbm))
    ]
    for read in reads:
        read.start()
    loads = {}
    order = [(q, c) for c in range(len(chunks)) for q in range(2)]
    order += [(2, c) for c in range(len(chunks))]
    for q, c in order:
        start, width = chunks[c]
        src = (wg_hbm, wu_hbm, wd_hbm)[q]
        loads[q, c] = pltpu.make_async_copy(
            src.at[pl.ds(start, width)], weights[q].at[pl.ds(start, width)], w_sem.at[q, c]
        )
        loads[q, c].start()

    barrier = pltpu.get_barrier_semaphore()
    for k in range(1, nz):
        pl.semaphore_signal(barrier, inc=1, device_id={"seq": z_at(k) * 2 + y}, device_id_type=MESH)
    for k in range(1, nchip):
        pl.semaphore_signal(barrier, inc=1, device_id={"tp": chip_at(k) * 2 + core}, device_id_type=MESH)
    pl.semaphore_signal(barrier, inc=1, device_id=at_y, device_id_type=MESH)
    pl.semaphore_signal(barrier, inc=1, device_id=at_core, device_id_type=MESH)
    for a in range(2):
        reads[a].wait()
        rows = [raw[a, b].astype(F32) for b in range(blocks)]
        own[a] = jnp.concatenate(rows, axis=0).astype(BF16)
    pl.semaphore_wait(barrier, nz - 1 + nchip - 1 + 2)

    def remote(src, dst, send, recv, to):
        return pltpu.make_async_remote_copy(
            src_ref=src, dst_ref=dst, send_sem=send, recv_sem=recv, device_id=to, device_id_type=MESH
        )

    z_copies, y_copies = [], []
    for a in range(2):
        z_copies.append([
            remote(own.at[a], gath.at[a, z, y], z_send.at[a, k], z_recv.at[a, k], {"seq": z_at(k) * 2 + y})
            for k in range(1, nz)
        ])
        over = [remote(own.at[a], gath.at[a, z, y], y_send.at[a, 0], y_recv.at[a, 0], at_y)]
        over += [
            remote(gath.at[a, z_at(nz - k), y], gath.at[a, z_at(nz - k), y],
                   y_send.at[a, k], y_recv.at[a, k], at_y)
            for k in range(1, nz)
        ]
        y_copies.append(over)
    for a in range(2):
        for copy in z_copies[a]:
            copy.start()
        y_copies[a][0].start()
    for a in range(2):
        gath[a, z, y] = own[a]

    def forward(a):
        for k in range(1, nz):
            z_copies[a][k - 1].wait_recv()
            y_copies[a][k].start()

    def arrive(a, out):
        for k in range(nz):
            y_copies[a][k].wait_recv()
        out[...] = gath[a].astype(F32).reshape(out.shape).astype(BF16)

    c_copies, r_copies, f_copies = {}, {}, {}
    for c, (start, width) in enumerate(chunks):
        columns = pl.ds(start, padded(width))
        for q in range(3):
            c_copies[q, c] = remote(
                part.at[q, 1 - core, :, columns], from_core.at[q, :, columns],
                c_send.at[q, c], c_recv.at[q, c], at_core,
            )
            r_copies[q, c] = [
                remote(sendx.at[q, :, columns], from_chip.at[q, k - 1, :, columns],
                       r_send.at[q, c, k], r_recv.at[q, c, k], {"tp": chip_at(k) * 2 + core})
                for k in range(1, nchip)
            ]
        mine = acts.at[core, :, :, columns]
        f_copies[c] = remote(mine, mine, f_send.at[c], f_recv.at[c], at_core)

    def product(q, c):
        start, width = chunks[c]
        loads[q, c].wait()
        left = (x_out, x_out, dy_out)[q]
        val = lax.dot_general(
            left[...], weights[q][pl.ds(start, width), :], NT, preferred_element_type=F32
        )
        part[q, :, :, pl.ds(start, width)] = val.reshape(2, half, width)
        c_copies[q, c].start()

    def reduce_chip(q, c):
        columns = pl.ds(chunks[c][0], padded(chunks[c][1]))
        c_copies[q, c].wait_recv()
        total = part[q, core, :, columns] + from_core[q, :, columns]
        sendx[q, :, columns] = total.astype(BF16)
        for copy in r_copies[q, c]:
            copy.start()

    def activate(c):
        columns = pl.ds(chunks[c][0], padded(chunks[c][1]))
        values = []
        for q in range(3):
            value = part[q, core, :, columns] + from_core[q, :, columns]
            for k in range(1, nchip):
                r_copies[q, c][k - 1].wait_recv()
                value = value + from_chip[q, k - 1, :, columns].astype(F32)
            values.append(value)
        gate, up, grad = values
        sig = jax.nn.sigmoid(gate)
        acts[core, 0, :, columns] = (grad * up * sig * (1.0 + gate * (1.0 - sig))).astype(BF16)
        acts[core, 1, :, columns] = (grad * gate * sig).astype(BF16)
        acts[core, 2, :, columns] = (gate * sig * up).astype(BF16)
        f_copies[c].start()

    def back(c):
        start, width = chunks[c]
        columns = pl.ds(start, width)
        f_copies[c].wait_recv()
        for q, out in enumerate((gu_out, uu_out, hid_out)):
            out[:, columns] = acts[:, q, :, columns].reshape(2 * half, width)
        val = jnp.dot(gu_out[:, columns], wg[columns, :], preferred_element_type=F32)
        val = val + jnp.dot(uu_out[:, columns], wu[columns, :], preferred_element_type=F32)
        if c:
            val = val + ig_out[...]
        ig_out[...] = val

    forward(0)
    forward(1)
    arrive(0, x_out)
    for i, (q, c) in enumerate(order):
        if (q, c) == (2, 0):
            arrive(1, dy_out)
        product(q, c)
        if i >= LAG:
            reduce_chip(*order[i - LAG])
    for q, c in order[-LAG:]:
        reduce_chip(q, c)
    for c in range(len(chunks)):
        activate(c)
        if c:
            back(c - 1)
    back(len(chunks) - 1)

    for a in range(2):
        for copy in z_copies[a] + y_copies[a]:
            copy.wait_send()
    for q, c in order:
        for copy in [c_copies[q, c]] + r_copies[q, c]:
            copy.wait_send()
    for c in range(len(chunks)):
        f_copies[c].wait_send()


def front(n_seq, n_tp, x, dy, wg, wu, wd):
    blocks, lines, width = x.shape
    rows = blocks * lines
    ffw = wg.shape[0]
    tokens = rows * n_seq
    nz, nchip = n_seq // 2, n_tp // 2
    half = tokens // 2
    cols = padded(ffw)
    n_chunks = len(chunks_of(ffw))
    others = max(nchip - 1, 1)
    vmem = pl.BlockSpec(memory_space=pltpu.VMEM)
    hbm = pl.BlockSpec(memory_space=pl.ANY)
    dma = pltpu.SemaphoreType.DMA
    return pl.pallas_call(
        functools.partial(front_kernel, n_seq, n_tp),
        out_shape=[jax.ShapeDtypeStruct((tokens, width), BF16)] * 2
        + [jax.ShapeDtypeStruct((tokens, ffw), BF16)] * 3
        + [jax.ShapeDtypeStruct((tokens, width), F32)],
        in_specs=[hbm] * 5,
        out_specs=[vmem] * 6,
        scratch_shapes=[
            pltpu.VMEM((2, blocks, lines, width), BF16),
            pltpu.VMEM((2, rows, width), BF16),
            pltpu.VMEM((2, nz, 2, rows, width), BF16),
            pltpu.VMEM(wg.shape, BF16),
            pltpu.VMEM(wu.shape, BF16),
            pltpu.VMEM(wd.shape, BF16),
            pltpu.VMEM((3, 2, half, cols), F32),
            pltpu.VMEM((3, half, cols), F32),
            pltpu.VMEM((3, half, cols), BF16),
            pltpu.VMEM((3, others, half, cols), BF16),
            pltpu.VMEM((2, 3, half, cols), BF16),
            dma((2,)),
            dma((3, n_chunks)),
            dma((2, nz)), dma((2, nz)), dma((2, nz)), dma((2, nz)),
            dma((3, n_chunks)), dma((3, n_chunks)),
            dma((3, n_chunks, nchip)), dma((3, n_chunks, nchip)),
            dma((n_chunks,)), dma((n_chunks,)),
        ],
        compiler_params=pltpu.CompilerParams(
            collective_id=0, has_side_effects=True, vmem_limit_bytes=48 * 1024 * 1024
        ),
        cost_estimate=pl.CostEstimate(
            flops=10 * tokens * width * ffw, bytes_accessed=6 * width * ffw, transcendentals=0
        ),
    )(x, dy, wg, wu, wd)


def block_of(rows):
    return max(r for r in range(16, 513, 16) if rows % r == 0)


def weight_kernel(pairs, slots, rows, *refs):
    lefts, rights = refs[:pairs], refs[pairs : 2 * pairs]
    outs = refs[2 * pairs : 3 * pairs]
    stage, sem = refs[3 * pairs :]
    copies = []
    for left, right, out in zip(lefts, rights, outs):
        for start in range(0, out.shape[0], rows):
            slot = len(copies) % slots
            if len(copies) >= slots:
                copies[-slots].wait()
            turned = left[:, pl.ds(start, rows)].astype(F32).T.astype(BF16)
            stage[slot] = jnp.dot(turned, right[...], preferred_element_type=F32)
            copy = pltpu.make_async_copy(stage.at[slot], out.at[pl.ds(start, rows)], sem.at[slot])
            copy.start()
            copies.append(copy)
    for copy in copies[-slots:]:
        copy.wait()


def weight_grads(lefts, rights):
    tokens, width = rights[0].shape
    ffw = lefts[0].shape[1]
    pairs = len(lefts)
    rows = block_of(ffw)
    slots = min(4, pairs * (ffw // rows))
    return pl.pallas_call(
        functools.partial(weight_kernel, pairs, slots, rows),
        out_shape=[jax.ShapeDtypeStruct((ffw, width), F32)] * pairs,
        in_specs=[pl.BlockSpec(memory_space=pltpu.VMEM)] * (2 * pairs),
        out_specs=[pl.BlockSpec(memory_space=pl.ANY)] * pairs,
        scratch_shapes=[
            pltpu.VMEM((slots, rows, width), F32),
            pltpu.SemaphoreType.DMA((slots,)),
        ],
        compiler_params=pltpu.CompilerParams(vmem_limit_bytes=32 * 1024 * 1024),
        cost_estimate=pl.CostEstimate(
            flops=16 * pairs * tokens * ffw * width,
            bytes_accessed=4 * pairs * ffw * width,
            transcendentals=0,
        ),
    )(*lefts, *rights)


def scatter_sum(n_seq, partial, cover):
    nz = n_seq // 2
    seq = lax.axis_index("seq")
    z, y = seq // 2, lax.rem(seq, 2)
    rows = partial.shape[0] // n_seq
    pieces = partial.reshape(nz, 2, rows, partial.shape[1])
    away = lax.dynamic_index_in_dim(pieces, 1 - y, 1, keepdims=False).astype(BF16)
    kept = lax.dynamic_index_in_dim(pieces, y, 1, keepdims=False)
    arrived = lax.ppermute(away, "seq", [(i, i ^ 1) for i in range(n_seq)])
    kept, *cover = lax.optimization_barrier((kept, *cover))
    summed = kept + arrived.astype(F32)
    result = lax.dynamic_index_in_dim(summed, z, 0, keepdims=False)
    for k in range(1, nz):
        send = lax.dynamic_index_in_dim(summed, lax.rem(z + k, nz), 0, keepdims=False).astype(BF16)
        arrived = lax.ppermute(send, "seq", [(i, (i + 2 * k) % n_seq) for i in range(n_seq)])
        result = result + arrived.astype(F32)
    return result, cover


def solution(mesh):
    n_seq, n_tp = mesh.shape["seq"], mesh.shape["tp"]

    def per_device(inputs, out_grad, gate_weight, up_weight, down_weight):
        x, dy, gate_unit, up_unit, hidden, partial = front(
            n_seq, n_tp, inputs, out_grad, gate_weight.T, up_weight.T, down_weight
        )
        cover = weight_grads((gate_unit,), (x,))
        total, (gate_grad,) = scatter_sum(n_seq, partial, cover)
        up_grad, down_grad = weight_grads((up_unit, hidden), (x, dy))
        return total.astype(BF16).reshape(inputs.shape), gate_grad.T, up_grad.T, down_grad

    return jax.shard_map(
        per_device,
        mesh=mesh,
        in_specs=(
            P(None, "seq", "tp"),
            P(None, "seq", "tp"),
            P("tp", "seq"),
            P("tp", "seq"),
            P("seq", "tp"),
        ),
        out_specs=(P(None, "seq", "tp"), P("tp", "seq"), P("tp", "seq"), P("seq", "tp")),
        check_vma=False,
    )
```

time: 69.9 us -> 58 us (0.83)
  Pallas kernels: 59.9 us -> 50.4 us
  local copies, waits for them, and re-layouts: 3.83 us -> 2.22 us
  starting transfers between devices: 5.13 us -> 4.34 us
    pallas_call x1, Pallas kernels: 39.3 us -> 33.3 us  [front(): pl.pallas_call(functools.partial(front_kernel, n_seq, n_tp), out_shape=[j...]
    pallas_call x2, Pallas kernels: 20.6 us -> 17.1 us  [weight_grads(): pl.pallas_call(functools.partial(weight_kernel, pairs, slots, rows), out_...]
    reshape x2 -> x0, local copies, waits for them, and re-layouts: 1.55 us -> none  [the longest x1 0.77 us: per_device(): out_grad.reshape(blocks * rows, width)]
    unnamed x10 -> x4, local copies, waits for them, and re-layouts: 1.58 us -> 1.51 us
where the time goes in v1:
time: 58 us; the launch traced here: 57.8 us
  Pallas kernels  50.4 us (87%)
  starting transfers between devices  4.34 us (7%)
  local copies, waits for them, and re-layouts  2.22 us (4%)
  between operations  0.77 us (1%)
    pallas_call x1, Pallas kernels, front(): pl.pallas_call(functools.partial(front_kernel, n_seq, n_tp), out_shape=[j...  33.3 us
    pallas_call x2, Pallas kernels, weight_grads(): pl.pallas_call(functools.partial(weight_kernel, pairs, slots, rows), out_...  17.1 us
    ppermute x3, starting transfers between devices, scatter_sum(): lax.ppermute(send, 'seq', [(i, (i + 2 * k) % n_seq) for i in range(n_seq)])  3.88 us
    unnamed x4, local copies, waits for them, and re-layouts  1.51 us
  transfers between devices with their start and end apart: 4, of which 0 were waited for; matrix products, arithmetic and copies ran while one was open for 0% of the time, Pallas kernels for 30%

profile of v1, /device:TPU:0, one launch (start us, length us, event | category | flops | bytes accessed | tf_op | source)
XLA Modules:
  0.0 57.8 jit_solution(11045049716228162111)
XLA Ops:
  0.6 0.0 copy-start
  0.6 0.7 %copy-done = bf16[2,4,2048]{2,1,0:T(4,128)(2,1)S(1)} copy-done((bf16[2,4,2048]{2,1,0:T(4,128)(2,1)S(1)}, bf16[2,4,2048]{2,1,0:T(4,128)(2,1)}, u32[]{:S(2)}) %copy-start) | copy-done | bytes 32792
  1.4 0.0 copy-start.1
  1.4 0.8 %copy-done.1 = bf16[2,4,2048]{2,1,0:T(4,128)(2,1)S(1)} copy-done((bf16[2,4,2048]{2,1,0:T(4,128)(2,1)S(1)}, bf16[2,4,2048]{2,1,0:T(4,128)(2,1)}, u32[]{:S(2)}) %copy-start.1) | copy-done | bytes 32792
  2.2 33.3 %shard_map.84 = (bf16[64,2048]{1,0:T(8,128)(2,1)S(1)}, bf16[64,2048]{1,0:T(8,128)(2,1)S(1)}, bf16[64,1856]{1,0:T(8,128)(2,1)S(1)}, bf16[64,1856]{1,0:T(8,128)(2,...) custom-call(bf16[2,4,2048]{2,1,0:T(4,128)(2,1)S(1)} %copy-done, bf16[2,4,2048]{2,1,0:T(4,128)(2,1)S(1)} %copy-done.1, ...), custom_call_target="tpu_custom_call" | custom-call | flops 2432696320 | bytes 22806528 | tf_op jit(solution)/shard_map/pallas_call | solution.py:216
  35.5 0.5 collective-permute-start
  36.0 6.3 %shard_map.85 = f32[1856,2048]{1,0:T(8,128)} custom-call(bf16[64,1856]{1,0:T(8,128)(2,1)S(1)} %get-tuple-element.15.refs_0_, bf16[64,2048]{1,0:T(8,128)(2,1)S(1)} %get-tuple-element.16.refs_1_.refs_2_), custom_call_target="tpu_custom_call" | custom-call | flops 3892314112 | bytes 15204352 | tf_op jit(solution)/shard_map/pallas_call | solution.py:280
  42.3 0.0 collective-permute-done
  42.4 0.8 %collective-permute-start.1 = (bf16[8,2048]{1,0:T(8,128)(2,1)S(1)}, bf16[8,2048]{1,0:T(8,128)(2,1)S(1)}, u32[]{:S(2)}, u32[]{:S(2)}) collective-permute-start(bf16[8,2048]{1,0:T(8,128)(2,1)S(1)} %get-tuple-element.24), channel_id=1, source_target_pairs={{0,8},{4,12},{8,16},{12,20},{16,24},{20,28},{24,0},{28,4},{1,9},{5... | collective-permute-start | bytes 98312 | tf_op jit(solution)/shard_map/ppermute | solution.py:312
  43.2 3.0 %collective-permute-start.3 = (bf16[8,2048]{1,0:T(8,128)(2,1)S(1)}, bf16[8,2048]{1,0:T(8,128)(2,1)S(1)}, u32[]{:S(2)}, u32[]{:S(2)}) collective-permute-start(bf16[8,2048]{1,0:T(8,128)(2,1)S(1)} %get-tuple-element.25), channel_id=1, source_target_pairs={{0,24},{4,28},{8,0},{12,4},{16,8},{20,12},{24,16},{28,20},{1,25},{... | collective-permute-start | bytes 98312 | tf_op jit(solution)/shard_map/ppermute | solution.py:312
  46.3 0.0 collective-permute-start.2
  46.3 10.8 %shard_map.86 = (f32[1856,2048]{1,0:T(8,128)}, f32[1856,2048]{1,0:T(8,128)}) custom-call(bf16[64,1856]{1,0:T(8,128)(2,1)S(1)} %get-tuple-element.19.refs_0_, bf16[64,1856]{1,0:T(8,128)(2,1)S(1)} %get-tuple-element.20.refs_1_, bf16[64,2048]{1,0:T(8,128)(2,1)S(1)} %get-tuple-element.16.refs_1_.refs_2_, bf16[64,2048]{1,0:T(8,128)(2,1)S(1)} %get-tuple-element.21.refs_3_), custom_call_target="tpu_custom_call" | custom-call | flops 7784628224 | bytes 30408704 | tf_op jit(solution)/shard_map/pallas_call | solution.py:280
  57.1 0.0 collective-permute-done.1
  57.1 0.0 collective-permute-done.3
  57.1 0.0 collective-permute-done.2
  57.2 0.6 %reshape.19 = bf16[2,4,2048]{2,1,0:T(4,128)(2,1)} reshape(bf16[8,2048]{1,0:T(8,128)(2,1)S(1)} %fusion.3) | data formatting | bytes 65536 | tf_op jit(solution)/shard_map/reshape | solution.py:327
  (5 shorter events, 0.1 us)
Async XLA Ops:
  0.6 0.8 %copy-start = (bf16[2,4,2048]{2,1,0:T(4,128)(2,1)S(1)}, bf16[2,4,2048]{2,1,0:T(4,128)(2,1)}, u32[]{:S(2)}) copy-start(bf16[2,4,2048]{2,1,0:T(4,128)(2,1)} %x_hbm.1) | copy-start | bytes 98308
  1.4 0.8 %copy-start.1 = (bf16[2,4,2048]{2,1,0:T(4,128)(2,1)S(1)}, bf16[2,4,2048]{2,1,0:T(4,128)(2,1)}, u32[]{:S(2)}) copy-start(bf16[2,4,2048]{2,1,0:T(4,128)(2,1)} %dy_hbm.1) | copy-start | bytes 98308
  35.5 6.8 %collective-permute-start = (bf16[4,8,2048]{2,1,0:T(8,128)(2,1)S(1)}, bf16[4,8,2048]{2,1,0:T(8,128)(2,1)S(1)}, u32[]{:S(2)}, u32[]{:S(2)}) collective-permute-start(bf16[4,8,2048]{2,1,0:T(8,128)(2,1)S(1)} %fusion), channel_id=1, source_target_pairs={{0,4},{4,0},{8,12},{12,8},{16,20},{20,16},{24,28},{28,24},{1,5},{5... | collective-permute-start | bytes 393224 | tf_op jit(solution)/shard_map/ppermute | solution.py:306
  42.4 14.7 %collective-permute-start.1 = (bf16[8,2048]{1,0:T(8,128)(2,1)S(1)}, bf16[8,2048]{1,0:T(8,128)(2,1)S(1)}, u32[]{:S(2)}, u32[]{:S(2)}) collective-permute-start(bf16[8,2048]{1,0:T(8,128)(2,1)S(1)} %get-tuple-element.24), channel_id=1, source_target_pairs={{0,8},{4,12},{8,16},{12,20},{16,24},{20,28},{24,0},{28,4},{1,9},{5... | collective-permute-start | bytes 98312 | tf_op jit(solution)/shard_map/ppermute | solution.py:312
  43.2 13.9 %collective-permute-start.3 = (bf16[8,2048]{1,0:T(8,128)(2,1)S(1)}, bf16[8,2048]{1,0:T(8,128)(2,1)S(1)}, u32[]{:S(2)}, u32[]{:S(2)}) collective-permute-start(bf16[8,2048]{1,0:T(8,128)(2,1)S(1)} %get-tuple-element.25), channel_id=1, source_target_pairs={{0,24},{4,28},{8,0},{12,4},{16,8},{20,12},{24,16},{28,20},{1,25},{... | collective-permute-start | bytes 98312 | tf_op jit(solution)/shard_map/ppermute | solution.py:312
  46.3 10.9 %collective-permute-start.2 = (bf16[8,2048]{1,0:T(8,128)(2,1)S(1)}, bf16[8,2048]{1,0:T(8,128)(2,1)S(1)}, u32[]{:S(2)}, u32[]{:S(2)}) collective-permute-start(bf16[8,2048]{1,0:T(8,128)(2,1)S(1)} %get-tuple-element.26), channel_id=1, source_target_pairs={{0,16},{4,20},{8,24},{12,28},{16,0},{20,4},{24,8},{28,12},{1,17},{... | collective-permute-start | bytes 98312 | tf_op jit(solution)/shard_map/ppermute | solution.py:312

commit v2 on v1

v2 whole, which is shorter than its diff:
```python
import functools

import jax
import jax.numpy as jnp
from jax import lax
from jax.experimental import pallas as pl
from jax.experimental.pallas import tpu as pltpu
from jax.sharding import PartitionSpec as P

MESH = pl.DeviceIdType.MESH
F32 = jnp.float32
BF16 = jnp.bfloat16
NT = (((1,), (1,)), ((), ()))
CHUNK = 512


def padded(size):
    return pl.cdiv(size, 128) * 128


def pieces_of(size, first):
    cuts, start, width = [], 0, first
    while start < size:
        if size - start - width < 128:
            width = size - start
        cuts.append((start, width))
        start, width = start + width, CHUNK
    return cuts


def chunks_of(ffw):
    return pieces_of(ffw, CHUNK)


def jobs_of(n):
    early, rest = range(min(2, n - 1)), range(min(2, n - 1), n - 1)
    jobs = [([(0, c), (1, c)], turn) for turn in range(2) for c in early]
    if n > 1:
        jobs.append(([(2, c) for c in early], 2))
    jobs += [([(0, c), (1, c)], 2) for c in rest]
    last = [(2, c) for c in rest] + [(0, n - 1), (1, n - 1)]
    return jobs + [(last, 2), ([(2, n - 1)], 2)]


def flipped(i, k, n):
    if n & (n - 1):
        return lax.rem(i + k, n)
    for bit in range(k.bit_length()):
        if k >> bit & 1:
            i = i + (1 - 2 * lax.rem(lax.div(i, 1 << bit), 2)) * (1 << bit)
    return i


def source(i, k, n):
    return flipped(i, n - k if n & (n - 1) else k, n)


def front_kernel(n_seq, n_tp, x_hbm, dy_hbm, wg_hbm, wu_hbm, wd_hbm,
                 x_out, dy_out, gu_out, uu_out, hid_out, ig_out,
                 raw, own, gath, wg, wu, wd, part, from_core, sendx, from_chip, acts, grads,
                 in_sem, w_sem, z_send, z_recv, y_send, y_recv,
                 c_send, c_recv, r_send, r_recv, f_send, f_recv):
    seq = lax.axis_index("seq")
    tp = lax.axis_index("tp")
    nz, nchip = n_seq // 2, n_tp // 2
    z, y = lax.div(seq, 2), lax.rem(seq, 2)
    chip, core = lax.div(tp, 2), lax.rem(tp, 2)
    blocks, lines = x_hbm.shape[:2]
    rows = blocks * lines
    ffw = wg_hbm.shape[0]
    half = gu_out.shape[0] // 2
    chunks = chunks_of(ffw)
    weights = (wg, wu, wd)
    at_y = {"seq": z * 2 + (1 - y)}
    at_core = {"tp": chip * 2 + (1 - core)}

    far_first = range(nz - 1, 0, -1)

    def z_at(k):
        return flipped(z, k, nz)

    def z_from(k):
        return source(z, k, nz)

    def chip_at(k):
        return lax.rem(chip + k, nchip)

    barrier = pltpu.get_barrier_semaphore()
    for k in range(1, nz):
        pl.semaphore_signal(barrier, inc=1, device_id={"seq": z_at(k) * 2 + y}, device_id_type=MESH)
    for k in range(1, nchip):
        pl.semaphore_signal(barrier, inc=1, device_id={"tp": chip_at(k) * 2 + core}, device_id_type=MESH)
    pl.semaphore_signal(barrier, inc=1, device_id=at_y, device_id_type=MESH)
    pl.semaphore_signal(barrier, inc=1, device_id=at_core, device_id_type=MESH)
    reads = [
        pltpu.make_async_copy(src, raw.at[a], in_sem.at[a]) for a, src in enumerate((x_hbm, dy_hbm))
    ]
    for read in reads:
        read.start()
    loads = {}
    jobs = jobs_of(len(chunks))
    order = [(q, c, turn) for items, turn in jobs for q, c in items]
    for q, c, turn in order:
        if turn == 1:
            continue
        start, width = chunks[c]
        src = (wg_hbm, wu_hbm, wd_hbm)[q]
        loads[q, c] = pltpu.make_async_copy(
            src.at[pl.ds(start, width)], weights[q].at[pl.ds(start, width)], w_sem.at[q, c]
        )
        loads[q, c].start(priority=1)


    def settle(a):
        reads[a].wait()
        values = [raw[a, b].astype(F32) for b in range(blocks)]
        own[a] = jnp.concatenate(values, axis=0).astype(BF16)

    settle(0)
    pl.semaphore_wait(barrier, nz - 1 + nchip - 1 + 2)

    def remote(src, dst, send, recv, to):
        return pltpu.make_async_remote_copy(
            src_ref=src, dst_ref=dst, send_sem=send, recv_sem=recv, device_id=to, device_id_type=MESH
        )

    z_copies, y_copies = [], []
    for a in range(2):
        z_copies.append({
            k: remote(own.at[a], gath.at[a, z, y], z_send.at[a, k], z_recv.at[a, k], {"seq": z_at(k) * 2 + y})
            for k in far_first
        })
        over = {0: remote(own.at[a], gath.at[a, z, y], y_send.at[a, 0], y_recv.at[a, 0], at_y)}
        for k in far_first:
            theirs = gath.at[a, z_from(k), y]
            over[k] = remote(theirs, theirs, y_send.at[a, k], y_recv.at[a, k], at_y)
        y_copies.append(over)

    def spread(a):
        for k in far_first:
            z_copies[a][k].start()
        y_copies[a][0].start()
        gath[a, z, y] = own[a]

    def forward(a):
        for k in far_first:
            z_copies[a][k].wait_recv()
            y_copies[a][k].start()

    def arrive(a, out):
        for k in range(nz):
            y_copies[a][k].wait_recv()
        out[...] = gath[a].astype(F32).reshape(out.shape).astype(BF16)

    pairs = nz // 2

    def lines_at(turn):
        return (y, 1 - y, slice(None))[turn]

    c_copies, r_copies, f_copies = {}, {}, {}
    for q, c, turn in order:
        columns = pl.ds(chunks[c][0], padded(chunks[c][1]))
        at = lines_at(turn)
        slot = turn % 2
        c_copies[q, c, turn] = remote(
            part.at[q, pl.ds((1 - core) * pairs, pairs), at, :, columns],
            from_core.at[q, :, at, :, columns],
            c_send.at[q, c, slot], c_recv.at[q, c, slot], at_core,
        )
        r_copies[q, c, turn] = [
            remote(sendx.at[q, :, at, :, columns], from_chip.at[q, k - 1, :, at, :, columns],
                   r_send.at[q, c, slot, k], r_recv.at[q, c, slot, k],
                   {"tp": chip_at(k) * 2 + core})
            for k in range(1, nchip)
        ]
    for c, (start, width) in enumerate(chunks):
        mine = acts.at[core, :, :, pl.ds(start, padded(width))]
        f_copies[c] = remote(mine, mine, f_send.at[c], f_recv.at[c], at_core)

    def multiply(items, turn):
        if turn != 1:
            for item in items:
                loads[item].wait()
        for q, c in items:
            columns = pl.ds(*chunks[c])
            at = lines_at(turn)
            if turn < 2:
                left = gath[q // 2, :, at].astype(F32).reshape(nz * rows, -1).astype(BF16)
            else:
                left = (x_out, x_out, dy_out)[q][...]
            val = lax.dot_general(left, weights[q][columns, :], NT, preferred_element_type=F32)
            shape = (nz, rows) if turn < 2 else (nz, 2, rows)
            part[q, :, at, :, columns] = val.reshape(*shape, chunks[c][1])
        for q, c in items:
            c_copies[q, c, turn].start()

    def reduce_chip(q, c, turn):
        columns = pl.ds(chunks[c][0], padded(chunks[c][1]))
        at = lines_at(turn)
        c_copies[q, c, turn].wait_recv()
        total = part[q, pl.ds(core * pairs, pairs), at, :, columns] + from_core[q, :, at, :, columns]
        sendx[q, :, at, :, columns] = total.astype(BF16)
        for copy in r_copies[q, c, turn]:
            copy.start()

    def activate(c):
        columns = pl.ds(chunks[c][0], padded(chunks[c][1]))
        for turn in range(3):
            for q in range(3):
                for copy in r_copies.get((q, c, turn), []):
                    copy.wait_recv()
        values = []
        for q in range(3):
            value = part[q, pl.ds(core * pairs, pairs), :, :, columns] + from_core[q, :, :, :, columns]
            for k in range(1, nchip):
                value = value + from_chip[q, k - 1, :, :, :, columns].astype(F32)
            values.append(value.reshape(half, -1))
        gate, up, grad = values
        sig = jax.nn.sigmoid(gate)
        acts[core, 0, :, columns] = (grad * up * sig * (1.0 + gate * (1.0 - sig))).astype(BF16)
        acts[core, 1, :, columns] = (grad * gate * sig).astype(BF16)
        acts[core, 2, :, columns] = (gate * sig * up).astype(BF16)
        f_copies[c].start()

    def back(c):
        start, width = chunks[c]
        columns = pl.ds(start, width)
        f_copies[c].wait_recv()
        for q, out in enumerate((gu_out, uu_out, hid_out)):
            out[:, columns] = acts[:, q, :, columns].reshape(2 * half, width)
        val = jnp.dot(gu_out[:, columns], wg[columns, :], preferred_element_type=F32)
        val = val + jnp.dot(uu_out[:, columns], wu[columns, :], preferred_element_type=F32)
        if c:
            val = val + grads[...]
        if c < len(chunks) - 1:
            grads[...] = val
            return
        for i in range(n_seq * blocks):
            ig_out[i // blocks, i % blocks] = val[i * lines : (i + 1) * lines]

    spread(0)
    settle(1)
    forward(0)
    spread(1)
    waiting = []
    late = [i for i, (_, turn) in enumerate(jobs) if turn][0]
    for i, (items, turn) in enumerate(jobs):
        if i == late:
            arrive(0, x_out)
            forward(1)
        if (2, 0) in items:
            arrive(1, dy_out)
        multiply(items, turn)
        for item in waiting:
            reduce_chip(*item)
        waiting = [(q, c, turn) for q, c in items]
    for item in waiting:
        reduce_chip(*item)
    for c in range(len(chunks)):
        activate(c)
        if c:
            back(c - 1)
    back(len(chunks) - 1)

    for a in range(2):
        for copy in [*z_copies[a].values(), *y_copies[a].values()]:
            copy.wait_send()
    for item in order:
        for copy in [c_copies[item]] + r_copies[item]:
            copy.wait_send()
    for c in range(len(chunks)):
        f_copies[c].wait_send()


def front(n_seq, n_tp, x, dy, wg, wu, wd):
    blocks, lines, width = x.shape
    rows = blocks * lines
    ffw = wg.shape[0]
    tokens = rows * n_seq
    nz, nchip = n_seq // 2, n_tp // 2
    half = tokens // 2
    cols = padded(ffw)
    n_chunks = len(chunks_of(ffw))
    others = max(nchip - 1, 1)
    vmem = pl.BlockSpec(memory_space=pltpu.VMEM)
    hbm = pl.BlockSpec(memory_space=pl.ANY)
    dma = pltpu.SemaphoreType.DMA
    return pl.pallas_call(
        functools.partial(front_kernel, n_seq, n_tp),
        out_shape=[jax.ShapeDtypeStruct((tokens, width), BF16)] * 2
        + [jax.ShapeDtypeStruct((tokens, ffw), BF16)] * 3
        + [jax.ShapeDtypeStruct((n_seq, blocks, lines, width), F32)],
        in_specs=[hbm] * 5,
        out_specs=[vmem] * 6,
        scratch_shapes=[
            pltpu.VMEM((2, blocks, lines, width), BF16),
            pltpu.VMEM((2, rows, width), BF16),
            pltpu.VMEM((2, nz, 2, rows, width), BF16),
            pltpu.VMEM(wg.shape, BF16),
            pltpu.VMEM(wu.shape, BF16),
            pltpu.VMEM(wd.shape, BF16),
            pltpu.VMEM((3, nz, 2, rows, cols), F32),
            pltpu.VMEM((3, nz // 2, 2, rows, cols), F32),
            pltpu.VMEM((3, nz // 2, 2, rows, cols), BF16),
            pltpu.VMEM((3, others, nz // 2, 2, rows, cols), BF16),
            pltpu.VMEM((2, 3, half, cols), BF16),
            pltpu.VMEM((tokens, width), F32),
            dma((2,)),
            dma((3, n_chunks)),
            dma((2, nz)), dma((2, nz)), dma((2, nz)), dma((2, nz)),
            dma((3, n_chunks, 2)), dma((3, n_chunks, 2)),
            dma((3, n_chunks, 2, nchip)), dma((3, n_chunks, 2, nchip)),
            dma((n_chunks,)), dma((n_chunks,)),
        ],
        compiler_params=pltpu.CompilerParams(
            collective_id=0, has_side_effects=True, vmem_limit_bytes=48 * 1024 * 1024
        ),
        cost_estimate=pl.CostEstimate(
            flops=10 * tokens * width * ffw, bytes_accessed=6 * width * ffw, transcendentals=0
        ),
    )(x, dy, wg, wu, wd)


def weight_kernel(pairs, slots, *refs):
    lefts, rights = refs[:pairs], refs[pairs : 2 * pairs]
    outs = refs[2 * pairs : 3 * pairs]
    stage, sem = refs[3 * pairs :]
    copies = []
    for left, right, out in zip(lefts, rights, outs):
        for start, rows in pieces_of(out.shape[0], CHUNK if copies else 128):
            slot = len(copies) % slots
            if len(copies) >= slots:
                copies[-slots].wait()
            turned = left[:, pl.ds(start, rows)].astype(F32).T.astype(BF16)
            stage[slot, pl.ds(0, rows)] = jnp.dot(turned, right[...], preferred_element_type=F32)
            copy = pltpu.make_async_copy(
                stage.at[slot, pl.ds(0, rows)], out.at[pl.ds(start, rows)], sem.at[slot]
            )
            copy.start()
            copies.append(copy)
    for copy in copies[-slots:]:
        copy.wait()


def weight_grads(lefts, rights):
    tokens, width = rights[0].shape
    ffw = lefts[0].shape[1]
    pairs = len(lefts)
    cuts = pieces_of(ffw, 128) + pieces_of(ffw, CHUNK) * (pairs - 1)
    slots = min(4, len(cuts))
    return pl.pallas_call(
        functools.partial(weight_kernel, pairs, slots),
        out_shape=[jax.ShapeDtypeStruct((ffw, width), F32)] * pairs,
        in_specs=[pl.BlockSpec(memory_space=pltpu.VMEM)] * (2 * pairs),
        out_specs=[pl.BlockSpec(memory_space=pl.ANY)] * pairs,
        scratch_shapes=[
            pltpu.VMEM((slots, max(rows for _, rows in cuts), width), F32),
            pltpu.SemaphoreType.DMA((slots,)),
        ],
        compiler_params=pltpu.CompilerParams(vmem_limit_bytes=32 * 1024 * 1024),
        cost_estimate=pl.CostEstimate(
            flops=16 * pairs * tokens * ffw * width,
            bytes_accessed=4 * pairs * ffw * width,
            transcendentals=0,
        ),
    )(*lefts, *rights)


def scatter_sum(n_seq, partial, cover):
    nz = n_seq // 2
    seq = lax.axis_index("seq")
    z, y = seq // 2, lax.rem(seq, 2)
    pieces = partial.reshape(nz, 2, *partial.shape[1:])
    away = lax.dynamic_index_in_dim(pieces, 1 - y, 1, keepdims=False).astype(BF16)
    kept = lax.dynamic_index_in_dim(pieces, y, 1, keepdims=False)
    arrived = lax.ppermute(away, "seq", [(i, i ^ 1) for i in range(n_seq)])
    kept, *cover = lax.optimization_barrier((kept, *cover))
    summed = kept + arrived.astype(F32)
    result = lax.dynamic_index_in_dim(summed, z, 0, keepdims=False)
    for k in range(1, nz):
        send = lax.dynamic_index_in_dim(summed, flipped(z, k, nz), 0, keepdims=False).astype(BF16)
        pairs = [
            (i, 2 * (i // 2 ^ k) + i % 2 if nz & (nz - 1) == 0 else (i + 2 * k) % n_seq)
            for i in range(n_seq)
        ]
        result = result + lax.ppermute(send, "seq", pairs).astype(F32)
    return result, cover


def solution(mesh):
    n_seq, n_tp = mesh.shape["seq"], mesh.shape["tp"]

    def per_device(inputs, out_grad, gate_weight, up_weight, down_weight):
        inputs, out_grad = (
            pltpu.with_memory_space_constraint(a, pltpu.HBM) for a in (inputs, out_grad)
        )
        x, dy, gate_unit, up_unit, hidden, partial = front(
            n_seq, n_tp, inputs, out_grad, gate_weight.T, up_weight.T, down_weight
        )
        cover = weight_grads((gate_unit,), (x,))
        total, (gate_grad,) = scatter_sum(n_seq, partial, cover)
        up_grad, down_grad = weight_grads((up_unit, hidden), (x, dy))
        return total.astype(BF16), gate_grad.T, up_grad.T, down_grad

    return jax.shard_map(
        per_device,
        mesh=mesh,
        in_specs=(
            P(None, "seq", "tp"),
            P(None, "seq", "tp"),
            P("tp", "seq"),
            P("tp", "seq"),
            P("seq", "tp"),
        ),
        out_specs=(P(None, "seq", "tp"), P("tp", "seq"), P("tp", "seq"), P("seq", "tp")),
        check_vma=False,
    )
```

time: 58 us -> 54.1 us (0.933)
  Pallas kernels: 50.4 us -> 48.3 us
  local copies, waits for them, and re-layouts: 2.22 us -> 0.13 us
  other arithmetic: 0.05 us -> 0.68 us
    pallas_call x1, Pallas kernels: 33.3 us -> 31.7 us  [front(): pl.pallas_call(functools.partial(front_kernel, n_seq, n_tp), out_shape=[j...]
    unnamed x4 -> x0, local copies, waits for them, and re-layouts: 1.51 us -> none
    convert_element_type x1, other arithmetic: 0.02 us -> 0.65 us  [per_device(): return (total.astype(BF16), gate_grad.T, up_grad.T, down_grad)]
    reshape x1 -> x0, local copies, waits for them, and re-layouts: 0.63 us -> none  [per_device(): total.astype(BF16).reshape(inputs.shape)]
  transfers between devices with their start and end apart: 4 -> 4, of which waited for: 0 -> 0; matrix products, arithmetic and copies ran while one was open for 0% -> 0% of each run, Pallas kernels for 30% -> 31%
where the time goes in v2:
time: 54.1 us; the launch traced here: 54 us
  Pallas kernels  48.3 us (89%)
  starting transfers between devices  4.13 us (8%)
  between operations  0.75 us (1%)
  other arithmetic  0.68 us (1%)
    pallas_call x1, Pallas kernels, front(): pl.pallas_call(functools.partial(front_kernel, n_seq, n_tp), out_shape=[j...  31.7 us
    pallas_call x2, Pallas kernels, weight_grads(): pl.pallas_call(functools.partial(weight_kernel, pairs, slots), out_shape=...  16.5 us
    ppermute x3, starting transfers between devices, scatter_sum(): result = result + lax.ppermute(send, 'seq', pairs).astype(F32)  3.55 us
  transfers between devices with their start and end apart: 4, of which 0 were waited for; matrix products, arithmetic and copies ran while one was open for 0% of the time, Pallas kernels for 31%

profile of v2, /device:TPU:0, one launch (start us, length us, event | category | flops | bytes accessed | tf_op | source)
XLA Modules:
  0.0 54.0 jit_solution(8737922140510752808)
XLA Ops:
  0.6 31.7 %shard_map.84 = (bf16[64,2048]{1,0:T(8,128)(2,1)S(1)}, bf16[64,2048]{1,0:T(8,128)(2,1)S(1)}, bf16[64,1856]{1,0:T(8,128)(2,1)S(1)}, bf16[64,1856]{1,0:T(8,128)(2,...) custom-call(bf16[2,4,2048]{2,1,0:T(4,128)(2,1)} %x_hbm.1, bf16[2,4,2048]{2,1,0:T(4,128)(2,1)} %dy_hbm.1, ...), custom_call_target="tpu_custom_call" | custom-call | flops 2432696320 | bytes 22806528 | tf_op jit(solution)/shard_map/pallas_call | solution.py:288
  32.4 0.1 fusion
  32.5 0.6 %collective-permute-start = (bf16[4,2,4,2048]{3,2,1,0:T(4,128)(2,1)S(1)}, bf16[4,2,4,2048]{3,2,1,0:T(4,128)(2,1)S(1)}, u32[]{:S(2)}, u32[]{:S(2)}) collective-permute-start(bf16[4,2,4,2048]{3,2,1,0:T(4,128)(2,1)S(1)} %fusion), channel_id=1, source_target_pairs={{0,4},{4,0},{8,12},{12,8},{16,20},{20,16},{24,28},{28,24},{1,5},{5... | collective-permute-start | bytes 393224 | tf_op jit(solution)/shard_map/ppermute | solution.py:376
  33.0 6.0 %shard_map.85 = f32[1856,2048]{1,0:T(8,128)} custom-call(bf16[64,1856]{1,0:T(8,128)(2,1)S(1)} %get-tuple-element.15.refs_0_, bf16[64,2048]{1,0:T(8,128)(2,1)S(1)} %get-tuple-element.16.refs_1_.refs_2_), custom_call_target="tpu_custom_call" | custom-call | flops 3892314112 | bytes 15204352 | tf_op jit(solution)/shard_map/pallas_call | solution.py:351
  39.0 0.0 collective-permute-done
  39.1 0.6 %collective-permute-start.1 = (bf16[2,4,2048]{2,1,0:T(4,128)(2,1)S(1)}, bf16[2,4,2048]{2,1,0:T(4,128)(2,1)S(1)}, u32[]{:S(2)}, u32[]{:S(2)}) collective-permute-start(bf16[2,4,2048]{2,1,0:T(4,128)(2,1)S(1)} %get-tuple-element.24), channel_id=1, source_target_pairs={{0,8},{4,12},{8,0},{12,4},{16,24},{20,28},{24,16},{28,20},{1,9},{5... | collective-permute-start | bytes 98312 | tf_op jit(solution)/shard_map/ppermute | solution.py:386
  39.8 1.8 %collective-permute-start.3 = (bf16[2,4,2048]{2,1,0:T(4,128)(2,1)S(1)}, bf16[2,4,2048]{2,1,0:T(4,128)(2,1)S(1)}, u32[]{:S(2)}, u32[]{:S(2)}) collective-permute-start(bf16[2,4,2048]{2,1,0:T(4,128)(2,1)S(1)} %get-tuple-element.25), channel_id=1, source_target_pairs={{0,24},{4,28},{8,16},{12,20},{16,8},{20,12},{24,0},{28,4},{1,25},{... | collective-permute-start | bytes 98312 | tf_op jit(solution)/shard_map/ppermute | solution.py:386
  41.6 1.1 %collective-permute-start.2 = (bf16[2,4,2048]{2,1,0:T(4,128)(2,1)S(1)}, bf16[2,4,2048]{2,1,0:T(4,128)(2,1)S(1)}, u32[]{:S(2)}, u32[]{:S(2)}) collective-permute-start(bf16[2,4,2048]{2,1,0:T(4,128)(2,1)S(1)} %get-tuple-element.26), channel_id=1, source_target_pairs={{0,16},{4,20},{8,24},{12,28},{16,0},{20,4},{24,8},{28,12},{1,17},{... | collective-permute-start | bytes 98312 | tf_op jit(solution)/shard_map/ppermute | solution.py:386
  42.7 10.6 %shard_map.86 = (f32[1856,2048]{1,0:T(8,128)}, f32[1856,2048]{1,0:T(8,128)}) custom-call(bf16[64,1856]{1,0:T(8,128)(2,1)S(1)} %get-tuple-element.19.refs_0_, bf16[64,1856]{1,0:T(8,128)(2,1)S(1)} %get-tuple-element.20.refs_1_, bf16[64,2048]{1,0:T(8,128)(2,1)S(1)} %get-tuple-element.16.refs_1_.refs_2_, bf16[64,2048]{1,0:T(8,128)(2,1)S(1)} %get-tuple-element.21.refs_3_), custom_call_target="tpu_custom_call" | custom-call | flops 7784628224 | bytes 30408704 | tf_op jit(solution)/shard_map/pallas_call | solution.py:351
  53.3 0.0 collective-permute-done.1
  53.3 0.0 collective-permute-done.3
  53.3 0.0 collective-permute-done.2
  53.3 0.7 %fusion.3 = bf16[2,4,2048]{2,1,0:T(4,128)(2,1)} fusion(bf16[2,4,2048]{2,1,0:T(4,128)(2,1)S(1)} %collective-permute-done.3, bf16[2,4,2048]{2,1,0:T(4,128)(2,1)S(1)} %collective-permute-done.2, bf16[2,4,2048]{2,1,0:T(4,128)(2,1)S(1)} %collective-permute-done.1, f32[4,2,4,2048]{3,2,1,0:T(4,128)S(1)} %bitcast.37, s32[]{:T(128)S(6)} %select_n.28), kind=kLoop, calls=%fused_computation.7 | loop fusion | flops 114688 | bytes 196612 | tf_op jit(solution)/shard_map/convert_element_type | solution.py:403
  (3 shorter events, 0.1 us)
Async XLA Ops:
  32.5 6.6 %collective-permute-start = (bf16[4,2,4,2048]{3,2,1,0:T(4,128)(2,1)S(1)}, bf16[4,2,4,2048]{3,2,1,0:T(4,128)(2,1)S(1)}, u32[]{:S(2)}, u32[]{:S(2)}) collective-permute-start(bf16[4,2,4,2048]{3,2,1,0:T(4,128)(2,1)S(1)} %fusion), channel_id=1, source_target_pairs={{0,4},{4,0},{8,12},{12,8},{16,20},{20,16},{24,28},{28,24},{1,5},{5... | collective-permute-start | bytes 393224 | tf_op jit(solution)/shard_map/ppermute | solution.py:376
  39.1 14.1 %collective-permute-start.1 = (bf16[2,4,2048]{2,1,0:T(4,128)(2,1)S(1)}, bf16[2,4,2048]{2,1,0:T(4,128)(2,1)S(1)}, u32[]{:S(2)}, u32[]{:S(2)}) collective-permute-start(bf16[2,4,2048]{2,1,0:T(4,128)(2,1)S(1)} %get-tuple-element.24), channel_id=1, source_target_pairs={{0,8},{4,12},{8,0},{12,4},{16,24},{20,28},{24,16},{28,20},{1,9},{5... | collective-permute-start | bytes 98312 | tf_op jit(solution)/shard_map/ppermute | solution.py:386
  39.8 13.5 %collective-permute-start.3 = (bf16[2,4,2048]{2,1,0:T(4,128)(2,1)S(1)}, bf16[2,4,2048]{2,1,0:T(4,128)(2,1)S(1)}, u32[]{:S(2)}, u32[]{:S(2)}) collective-permute-start(bf16[2,4,2048]{2,1,0:T(4,128)(2,1)S(1)} %get-tuple-element.25), channel_id=1, source_target_pairs={{0,24},{4,28},{8,16},{12,20},{16,8},{20,12},{24,0},{28,4},{1,25},{... | collective-permute-start | bytes 98312 | tf_op jit(solution)/shard_map/ppermute | solution.py:386
  41.6 11.7 %collective-permute-start.2 = (bf16[2,4,2048]{2,1,0:T(4,128)(2,1)S(1)}, bf16[2,4,2048]{2,1,0:T(4,128)(2,1)S(1)}, u32[]{:S(2)}, u32[]{:S(2)}) collective-permute-start(bf16[2,4,2048]{2,1,0:T(4,128)(2,1)S(1)} %get-tuple-element.26), channel_id=1, source_target_pairs={{0,16},{4,20},{8,24},{12,28},{16,0},{20,4},{24,8},{28,12},{1,17},{... | collective-permute-start | bytes 98312 | tf_op jit(solution)/shard_map/ppermute | solution.py:386
